TPU v7x, 32 devices: a whole 2x2x4 slice. The times are simulated.
32 devices in a mesh: row: 8 (over z, x), col: 4 (over y, core).
Axes of the slice: x: 2, y: 2, z: 4, core: 2. Of those that a mesh axis runs over, the one named last changes fastest.
Arguments:
- gradients: bfloat16 [32, 1024, 5120], P(('row', 'col')), may hold values from -24 to 24
- bucket_lengths: int32 [16], replicated, may hold values from 1 to 128, 1024 in all
- owner_offset: int32 [8], replicated, may hold values from 0 to 3
- clip_rms: float32 [1], replicated, may hold values from 0.15 to 0.4
Outputs:
- clipped_shard: float32 [1024, 5120], P('row', 'col')
- bucket_rms: float32 [16], replicated
Inputs may be any that keep to these rules, and one draw needn't show every extreme that they name: `bucket_lengths`: the buckets cover all 1024 rows; the largest has exactly 128 rows.
All inputs are finite; a program needn't handle non-finite values.
Results may differ from a plain program's by a relative error of at most 0.0003.
Values sent between devices are 32-bit elements; how exact they have to be, the bound alone decides.
A program may use at most 128 MiB of HBM per device.

v0:
```python
import jax
import jax.numpy as jnp
from jax import lax
from jax.sharding import PartitionSpec as P


def turn_block(block, shift):
    return jnp.roll(block, -shift, axis=1)


def shards(gradients, bucket_lengths, owner_offset, clip_rms):
    n_row = lax.axis_size("row")
    n_col = lax.axis_size("col")
    devices = n_row * n_col
    source = gradients[0]
    total_rows, width = source.shape
    width_local = width // n_col
    rows_local = total_rows // n_row
    row_index = lax.axis_index("row")
    blocks = source.reshape(n_row, rows_local, n_col, width_local)
    blocks = jax.vmap(turn_block)(blocks, owner_offset)
    blocks = (
        blocks.transpose(0, 2, 1, 3).reshape(devices * rows_local, width_local).astype(jnp.float32)
    )
    summed = lax.psum_scatter(blocks, ("row", "col"), scatter_dimension=0, tiled=True)
    averaged = summed / devices
    ends = jnp.cumsum(bucket_lengths)
    starts = ends - bucket_lengths
    row_ids = row_index * rows_local + jnp.arange(rows_local, dtype=jnp.int32)
    member = ((row_ids[:, None] >= starts[None, :]) & (row_ids[:, None] < ends[None, :])).astype(
        jnp.float32
    )
    row_squares = jnp.sum(averaged * averaged, axis=1)
    local_squares = jnp.sum(row_squares[:, None] * member, axis=0)
    bucket_squares = lax.psum(local_squares, ("row", "col"))
    overall = jnp.sqrt(jnp.sum(bucket_squares) / (total_rows * width))
    factor = clip_rms[0] / jnp.maximum(overall, clip_rms[0])
    clipped_shard = averaged * factor
    bucket_rms = jnp.sqrt(bucket_squares / (bucket_lengths.astype(jnp.float32) * width))
    return (clipped_shard, bucket_rms)


def solution(mesh):
    in_specs = (P(("row", "col"), None, None), P(), P(), P())
    out_specs = (P("row", "col"), P())
    return jax.shard_map(shards, mesh=mesh, in_specs=in_specs, out_specs=out_specs, check_vma=False)
```

profile of v0, /device:TPU:0, one launch (start us, length us, event | category | flops | bytes accessed | tf_op | source)
XLA Modules:
  0.0 363.9 jit_solution(11172365279284914420)
XLA Ops:
  7.2 0.0 reduce-scatter.2.cloned.1.call-start
  7.2 19.4 %reshape.50 = bf16[8,128,4,1280]{3,2,1,0:T(4,128)(2,1)} reshape(bf16[1,1024,5120]{2,1,0:T(8,128)(2,1)} %param.4) | data formatting | bytes 20971520 | tf_op jit(solution)/shard_map/reshape;squeeze | solution.py:20
  26.6 9.8 %copy.12 = bf16[8,128,4,1280]{3,1,0,2:T(8,128)(2,1)} copy(bf16[8,128,4,1280]{3,2,1,0:T(4,128)(2,1)} %reshape.50) | data formatting | bytes 20971520 | tf_op jit(solution)/shard_map/reshape;squeeze | solution.py:20
  36.4 0.0 copy-start.1
  36.4 17.5 %pad_maximum_fusion = bf16[8,128,8,1280]{3,1,0,2:T(8,128)(2,1)} fusion(bf16[8,128,4,1280]{3,1,0,2:T(8,128)(2,1)} %copy.12), kind=kLoop, calls=%fused_computation.1 | loop fusion | flops 10485760 | bytes 31457280 | tf_op jit(solution)/shard_map/vmap(jit(_roll_dynamic))/concatenate | solution.py:8
  53.9 0.0 copy-done.1
  54.0 12.7 %gather_fusion = bf16[8,128,4,1280]{3,1,2,0:T(8,128)(2,1)} fusion(bf16[8,128,8,1280]{3,1,0,2:T(8,128)(2,1)} %pad_maximum_fusion, s32[8]{0:T(128)S(1)} %fusion.2), kind=kCustom, calls=%fused_computation | custom fusion | bytes 20971648 | tf_op jit(solution)/shard_map/vmap(jit(_roll_dynamic))/gather | solution.py:8
  66.6 13.6 %convert_element_type.18 = f32[8,128,4,1280]{3,1,2,0:T(8,128)} convert(bf16[8,128,4,1280]{3,1,2,0:T(8,128)(2,1)} %gather_fusion) | non-fusion elementwise | flops 5242880 | bytes 31457280 | tf_op jit(solution)/shard_map/convert_element_type | solution.py:23
  80.2 0.0 copy-start
  80.2 0.0 reduce-scatter.2.cloned.1.call-update
  80.3 0.6 copy-done
  80.9 0.1 copy.14
  81.0 0.1 reduce
  81.1 227.2 %reduce-scatter.2.cloned.1.call-done = f32[128,1280]{1,0:T(8,128)} async-done(((f32[4096,1280]{1,0:T(8,128)}), f32[128,1280]{1,0:T(8,128)}) %reduce-scatter.2.cloned.1.call-update) | async-done | bytes 655376 | tf_op jit(solution)/shard_map/reduce_scatter | solution.py:25
  308.3 1.2 multiply_reduce_fusion
  309.6 0.2 select_reduce_fusion
  310.4 42.7 %psum.7 = f32[16]{0:T(128)S(1)} all-reduce(f32[16]{0:T(128)S(1)} %select_reduce_fusion), channel_id=1, replica_groups=mesh['row'=8,'col'=4] {'row','col'}, use_global_device_ids=true, to_apply=%region_4.5 | all-reduce | flops 16 | bytes 128 | tf_op jit(solution)/shard_map/psum | solution.py:35
  353.1 1.2 fusion.3
  355.1 2.0 broadcast_multiply_fusion
  (4 shorter events, 0.1 us)
Async XLA Ops:
  7.2 301.2 %reduce-scatter.2.cloned.1.call-start = ((), (), s32[]{:S(2)}) async-start(), calls=%async_computation.1 | async-start | bytes 21626880 | tf_op jit(solution)/shard_map/reduce_scatter | solution.py:25
  36.4 17.5 %copy-start.1 = (s32[8]{0:T(128)S(1)}, s32[8]{0:T(128)}, u32[]{:S(2)}) copy-start(s32[8]{0:T(128)} %param.6) | copy-start | bytes 100
  80.2 0.7 copy-start
Sparse Core Ops, SparseCore 0:
  80.4 227.9 reduce-scatter.1
where the time goes:
time: 365 us; the launch traced here: 364 us
  waiting for transfers between devices  227 us (62%)
  blocking collectives  42.7 us (12%)
  local copies, waits for them, and re-layouts  42.6 us (12%)
  other arithmetic  35.9 us (10%)
  between operations  15.5 us (4%)
    reduce_scatter x1, waiting for transfers between devices, shards(): lax.psum_scatter(blocks, ('row', 'col'), scatter_dimension=0, tiled=True)  227 us
    psum x1, blocking collectives, shards(): bucket_squares = lax.psum(local_squares, ('row', 'col'))  42.7 us
    another operation x2, local copies, waits for them, and re-layouts, shards(): blocks = source.reshape(n_row, rows_local, n_col, width_local)  29.2 us
    concatenate x1, other arithmetic, turn_block(): return jnp.roll(block, -shift, axis=1)  17.5 us
    convert_element_type x1, other arithmetic, shards(): blocks.transpose(0, 2, 1, 3).reshape(devices * rows_local, width_local)  13.6 us
    gather x1, local copies, waits for them, and re-layouts, turn_block(): return jnp.roll(block, -shift, axis=1)  12.7 us
  transfers between devices with their start and end apart: 1, of which 1 were waited for; matrix products, arithmetic and copies ran while one was open for 0% of the time, Pallas kernels for 0%

commit v1 on v0

v1 whole, which is shorter than its diff:
```python
import functools

import jax
import jax.numpy as jnp
from jax import lax
from jax.experimental import pallas as pl
from jax.experimental.pallas import tpu as pltpu
from jax.sharding import PartitionSpec as P

MESH = pl.DeviceIdType.MESH
F32 = jnp.float32


def kernel(
    n_row, n_col, g_ref, bounds_ref, pick_ref, clip_ref, avg_ref, fac_ref, rms_ref,
    src, send0, recv0, recv1, recv2, recv3, mine, slots, sq,
    load_sem, s0, r0, s1, r1, s2, r2, s3, r3, sa, ra,
):
    steps = recv0.shape[0]
    depth = n_row // 2
    devices = n_row * n_col
    total_rows, width = src.shape
    rows, w = total_rows // n_row, width // n_col
    row, col = lax.axis_index("row"), lax.axis_index("col")
    z, x = row // 2, row % 2
    y, core = col // 2, col % 2
    me = row * n_col + col
    core_peer = (row, y * 2 + 1 - core)
    peers = ((z * 2 + 1 - x, col), (row, (1 - y) * 2 + core))

    def place(k):
        other = (me + k) % devices
        return (other // n_col, other % n_col)

    def load(i):
        part = pl.ds(pl.multiple_of(i * rows, 16), rows)
        return pltpu.make_async_copy(g_ref.at[0, part], src.at[part], load_sem.at[i])

    def remote(a, b, s, r, dev):
        return pltpu.make_async_remote_copy(
            src_ref=a, dst_ref=b, send_sem=s, recv_sem=r, device_id=dev, device_id_type=MESH
        )

    def copy0(t, o):
        return remote(send0.at[t, o], recv0.at[t, o], s0.at[t, o], r0.at[t, o], core_peer)

    def copy1(t, o):
        return remote(recv0.at[t, o, 1], recv1.at[t, o], s1.at[t, o], r1.at[t, o], peers[o])

    def copy2(t, o):
        return remote(recv1.at[t, o, 1], recv2.at[t, o], s2.at[t, o], r2.at[t, o], peers[1 - o])

    def copy3(t, o, k):
        other = (z + k) % depth
        return remote(
            recv2.at[t, o, other], recv3.at[t, o, k - 1], s3.at[t, o, k - 1], r3.at[t, o, k - 1],
            (other * 2 + x, col),
        )

    def copya(k):
        return remote(mine, slots.at[me], sa.at[k], ra.at[me], place(k))

    for i in range(n_row):
        load(i).start()
    barrier = pltpu.get_barrier_semaphore()

    @pl.loop(1, devices)
    def _(k):
        pl.semaphore_signal(barrier, inc=1, device_id=place(k), device_id_type=MESH)

    pl.semaphore_wait(barrier, devices - 1)
    for i in range(n_row):
        load(i).wait()

    def piece(t, xr, yr, zi, to):
        r = zi * 2 + (x + xr) % 2
        c = ((y + yr) % 2) * 2 + to
        at = pl.ds(pl.multiple_of(r * rows + t * 16, 16), 16)
        total = None
        for j in range(n_col):
            weight = jnp.full((16, w), pick_ref[(r * n_col + c) * n_col + j], F32)
            term = src[at, j * w:(j + 1) * w] * weight.astype(src.dtype)
            total = term if total is None else total + term
        return total.astype(F32)

    def convert(t):
        for xr in (1, 0):
            for yr in (1, 0):
                @pl.loop(0, depth)
                def _(zi):
                    v = piece(t, xr, yr, zi, 1 - core)
                    send0[t, 0, xr, yr, zi] = v[:8]
                    send0[t, 1, yr, xr, zi] = v[8:]
        for o in range(2):
            copy0(t, o).start()

    def stage0(t):
        for o in range(2):
            copy0(t, o).wait_recv()
        for xr in (1, 0):
            for yr in (1, 0):
                @pl.loop(0, depth)
                def _(zi):
                    v = piece(t, xr, yr, zi, core)
                    recv0[t, 0, xr, yr, zi] += v[:8]
                    recv0[t, 1, yr, xr, zi] += v[8:]
        for o in range(2):
            copy1(t, o).start()

    def stage1(t):
        for o in range(2):
            copy1(t, o).wait_recv()
            for d in (1, 0):
                @pl.loop(0, depth)
                def _(zi):
                    recv1[t, o, d, zi] += recv0[t, o, 0, d, zi]
            copy2(t, o).start()

    def stage2(t):
        for o in range(2):
            copy2(t, o).wait_recv()

            @pl.loop(0, depth)
            def _(zi):
                recv2[t, o, zi] += recv1[t, o, 0, zi]

            for k in range(1, depth):
                copy3(t, o, k).start()

    def stage3(t):
        for o in range(2):
            v = recv2[t, o, z]
            for k in range(1, depth):
                copy3(t, o, k).wait_recv()
                v = v + recv3[t, o, k - 1]
            v = v * (1.0 / devices)
            at = pl.ds(pl.multiple_of(t * 16 + o * 8, 8), 8)
            avg_ref[at, :] = v
            v = v * v
            part = v[:, 0:128]
            for j in range(128, w, 128):
                part = part + v[:, j:j + 128]
            sq[at, :] = part

    stages = (convert, stage0, stage1, stage2, stage3)

    @pl.loop(0, steps + len(stages) - 1)
    def _(t):
        for lag, stage in enumerate(stages):
            @pl.when((t >= lag) & (t < steps + lag))
            def _():
                stage(t - lag)

    ids = lax.broadcasted_iota(jnp.int32, (rows, 128), 0) + row * rows
    starts, ends = bounds_ref[0:1, :], bounds_ref[1:2, :]
    after = jnp.clip(ids - starts + 1, 0, 1)
    before = jnp.clip(ends - ids, 0, 1)
    inside = (after * before).astype(F32)
    row_squares = jnp.sum(sq[...], axis=1, keepdims=True)
    local = jnp.sum(inside * row_squares, axis=0, keepdims=True)
    mine[...] = jnp.broadcast_to(local, mine.shape)
    slots[me] = jnp.broadcast_to(local, mine.shape)

    @pl.loop(1, devices)
    def _(k):
        copya(k).start()

    @pl.loop(0, steps)
    def _(t):
        for o in range(2):
            copy0(t, o).wait_send()
            copy1(t, o).wait_send()
            copy2(t, o).wait_send()
            for k in range(1, depth):
                copy3(t, o, k).wait_send()

    @pl.loop(1, devices)
    def _(k):
        other = (me + devices - k) % devices
        remote(mine, slots.at[other], sa.at[k], ra.at[other], place(k)).wait_recv()
        copya(k).wait_send()

    squares = lax.fori_loop(
        0, devices, lambda i, a: a + slots[i], jnp.zeros(mine.shape, F32)
    )
    overall = jnp.sqrt(jnp.sum(squares, axis=1, keepdims=True) / (total_rows * width))
    clip = clip_ref[0]
    fac_ref[...] = jnp.broadcast_to(clip / jnp.maximum(overall, clip), fac_ref.shape)
    safe = jnp.maximum(ends - starts, 1).astype(F32) * width
    rms_ref[...] = jnp.sqrt(squares / safe)


def shards(n_row, n_col, gradients, bucket_lengths, owner_offset, clip_rms):
    _, total_rows, width = gradients.shape
    rows, w = total_rows // n_row, width // n_col
    devices = n_row * n_col
    steps, depth = rows // 16, n_row // 2
    vmem, smem = pltpu.VMEM, pltpu.SMEM
    dma = pltpu.SemaphoreType.DMA
    ends = jnp.cumsum(bucket_lengths)
    bounds = jnp.stack([ends - bucket_lengths, ends])
    bounds = jnp.pad(bounds, ((0, 6), (0, 128 - bucket_lengths.shape[0])))
    block = jnp.arange(n_col, dtype=jnp.int32)
    origin = (block[None, :] + owner_offset[:, None]) % n_col
    pick = (origin[:, :, None] == block[None, None, :]).astype(F32).reshape(-1)
    averaged, factor, rms = pl.pallas_call(
        functools.partial(kernel, n_row, n_col),
        out_shape=(
            jax.ShapeDtypeStruct((rows, w), F32),
            jax.ShapeDtypeStruct((8, 128), F32),
            jax.ShapeDtypeStruct((8, 128), F32),
        ),
        in_specs=[
            pl.BlockSpec(memory_space=pl.ANY),
            pl.BlockSpec(memory_space=vmem),
            pl.BlockSpec(memory_space=smem),
            pl.BlockSpec(memory_space=smem),
        ],
        out_specs=[pl.BlockSpec(memory_space=vmem)] * 3,
        scratch_shapes=[
            vmem((total_rows, width), gradients.dtype),
            vmem((steps, 2, 2, 2, depth, 8, w), F32),
            vmem((steps, 2, 2, 2, depth, 8, w), F32),
            vmem((steps, 2, 2, depth, 8, w), F32),
            vmem((steps, 2, depth, 8, w), F32),
            vmem((steps, 2, depth - 1, 8, w), F32),
            vmem((8, 128), F32),
            vmem((devices, 8, 128), F32),
            vmem((rows, 128), F32),
            dma((n_row,)),
            dma((steps, 2)), dma((steps, 2)),
            dma((steps, 2)), dma((steps, 2)),
            dma((steps, 2)), dma((steps, 2)),
            dma((steps, 2, depth - 1)), dma((steps, 2, depth - 1)),
            dma((devices,)), dma((devices,)),
        ],
        compiler_params=pltpu.CompilerParams(
            collective_id=0, has_side_effects=True, vmem_limit_bytes=60 * 1024 * 1024
        ),
    )(gradients, bounds, pick, clip_rms)
    return averaged * factor[0, 0], rms[0, : bucket_lengths.shape[0]]


def solution(mesh):
    n_row, n_col = mesh.shape["row"], mesh.shape["col"]
    in_specs = (P(("row", "col"), None, None), P(), P(), P())
    out_specs = (P("row", "col"), P())
    return jax.shard_map(
        functools.partial(shards, n_row, n_col),
        mesh=mesh, in_specs=in_specs, out_specs=out_specs, check_vma=False,
    )
```

time: 365 us -> 129 us (0.35)
  waiting for transfers between devices: 227 us -> 0 us
  Pallas kernels: 0 us -> 119 us
  blocking collectives: 42.7 us -> 0 us
  local copies, waits for them, and re-layouts: 42.6 us -> 4.33 us
  other arithmetic: 35.9 us -> 4.24 us
  between operations: 15.5 us -> 1.29 us
    reduce_scatter x1 -> x0, waiting for transfers between devices: 227 us -> none  [shards(): lax.psum_scatter(blocks, ('row', 'col'), scatter_dimension=0, tiled=True)]
    pallas_call x0 -> x1, Pallas kernels: none -> 119 us  [shards(): pl.pallas_call(functools.partial(kernel, n_row, n_col), out_shape=(jax.Sh...]
    psum x1 -> x0, blocking collectives: 42.7 us -> none  [shards(): bucket_squares = lax.psum(local_squares, ('row', 'col'))]
    another operation x3 -> x0, local copies, waits for them, and re-layouts: 29.3 us -> none  [the longest x2 29.2 us: shards(): blocks = source.reshape(n_row, rows_local, n_col, width_local)]
    concatenate x1 -> x0, other arithmetic: 17.5 us -> none  [turn_block(): return jnp.roll(block, -shift, axis=1)]
    convert_element_type x1, other arithmetic: 13.6 us -> 0.07 us  [shards(): pick = (origin[:, :, None] == block[None, None, :]).astype(F32).reshape(-1)]
    gather x1 -> x0, local copies, waits for them, and re-layouts: 12.7 us -> none  [turn_block(): return jnp.roll(block, -shift, axis=1)]
  transfers between devices with their start and end apart: 1 -> 0, of which waited for: 1 -> 0; matrix products, arithmetic and copies ran while one was open for 0% -> 0% of each run, Pallas kernels for 0% -> 0%
where the time goes in v1:
time: 129 us
  Pallas kernels  119 us (92%)
  local copies, waits for them, and re-layouts  4.33 us (3%)
  other arithmetic  4.24 us (3%)
  between operations  1.29 us (1%)
    pallas_call x1, Pallas kernels, shards(): pl.pallas_call(functools.partial(kernel, n_row, n_col), out_shape=(jax.Sh...  119 us
    mul x1, other arithmetic, shards(): return (averaged * factor[0, 0], rms[0, :bucket_lengths.shape[0]])  2.61 us

profile of v1, /device:TPU:0, one launch (start us, length us, event | category | flops | bytes accessed | tf_op | source)
XLA Modules:
  0.0 128.7 jit_solution(5448256493876746956)
XLA Ops:
  1.3 0.7 add_select_fusion
  2.0 0.7 copy.7
  2.8 0.1 reduce
  2.9 0.7 subtract_bitcast_fusion
  3.6 0.6 pad.4.bounds_ref
  4.2 0.1 fusion
  4.2 0.6 reshape.51.pick_ref
  4.9 118.8 %shard_map.59 = (f32[128,1280]{1,0:T(8,128)}, f32[8,128]{1,0:T(8,128)}, f32[8,128]{1,0:T(8,128)}) custom-call(bf16[1,1024,5120]{2,1,0:T(8,128)(2,1)} %g_ref.1, s32[8,128]{1,0:T(8,128)} %pad.4.bounds_ref, f32[128]{0:T(128)} %reshape.51.pick_ref, f32[1]{0:T(128)S(6)} %copy.8.clip_ref), custom_call_target="tpu_custom_call" | custom-call | tf_op jit(solution)/shard_map/pallas_call | solution.py:206
  123.7 1.2 slice.6
  124.9 2.6 %broadcast_multiply_fusion = f32[128,1280]{1,0:T(8,128)} fusion(f32[128,1280]{1,0:T(8,128)} %get-tuple-element.5, f32[]{:T(128)} %bitcast.2), kind=kLoop, calls=%fused_computation | loop fusion | flops 163840 | bytes 1310724 | tf_op jit(solution)/shard_map/mul | solution.py:241
  127.5 1.2 slice_bitcast_fusion
  (2 shorter events, 0.0 us)

commit v2 on v0

v2 whole, which is shorter than its diff:
```python
import functools

import jax
import jax.numpy as jnp
from jax import lax
from jax.experimental import pallas as pl
from jax.experimental.pallas import tpu as pltpu
from jax.sharding import PartitionSpec as P

MESH = pl.DeviceIdType.MESH
F32 = jnp.float32
PARTS = 2
LAG = 2
ROWS = 16


def kernel(n_row, n_col, bits, g_ref, len_ref, off_ref, clip_ref, out_ref, rms_ref, src, send0, *rest):
    sums, rest = rest[: bits + 1], rest[bits + 1 :]
    mine, slots, sq, load_sem, sends, recvs, sa, ra = rest
    steps = send0.shape[0]
    blocks = 1 << bits
    devices = n_row * n_col
    _, rows, width = src.shape
    w = width // n_col
    part = w // PARTS
    row, col = lax.axis_index("row"), lax.axis_index("col")
    z, x = row // 2, row % 2
    y, core = col // 2, col % 2
    me = row * n_col + col

    def flip(value, bit):
        return value + (1 - 2 * ((value >> bit) % 2)) * (1 << bit)

    x_peer, y_peer = (flip(row, 0), col), (row, flip(col, 1))
    z_peers = [(flip(row, 1 + b), col) for b in range(bits - 2)]
    order = (
        [(row, flip(col, 0)), x_peer, z_peers[0], y_peer] + z_peers[1:],
        [(row, flip(col, 0)), y_peer, z_peers[0], x_peer] + z_peers[1:],
    )

    def place(k):
        other = (me + k) % devices
        return (other // n_col, other % n_col)

    def load(i):
        at = pl.ds(pl.multiple_of(i * ROWS, ROWS), ROWS)
        return pltpu.make_async_copy(g_ref.at[:, at], src.at[:, at], load_sem.at[i])

    def remote(a, b, s, r, dev):
        return pltpu.make_async_remote_copy(
            src_ref=a, dst_ref=b, send_sem=s, recv_sem=r, device_id=dev, device_id_type=MESH
        )

    def copy(stage, t, o):
        half = blocks >> stage
        a = send0.at[t, o] if stage == 0 else sums[stage - 1].at[t, o, pl.ds(half, half)]
        return remote(
            a, sums[stage].at[t, o], sends.at[stage, t, o], recvs.at[stage, t, o], order[o][stage]
        )

    def copya(k):
        return remote(mine, slots.at[me], sa.at[k], ra.at[me], place(k))

    @pl.loop(0, rows // ROWS)
    def _(i):
        load(i).start()

    barrier = pltpu.get_barrier_semaphore()

    @pl.loop(1, devices)
    def _(k):
        pl.semaphore_signal(barrier, inc=1, device_id=place(k), device_id_type=MESH)

    pl.semaphore_wait(barrier, devices - 1)

    def spot(i):
        xr, zr, yr = i >> (bits - 1), (i >> (bits - 2)) % 2, (i >> (bits - 3)) % 2
        low = i % (1 << (bits - 3))
        other = (
            (yr << (bits - 1)) + (zr << (bits - 2)) + (xr << (bits - 3)) + low
        )
        zd = (z + zr) % 2
        for b in range(1, bits - 2):
            zd = zd + ((((z >> b) + (low >> (bits - 3 - b))) % 2) << b)
        return zd * 2 + (x + xr) % 2, (y + yr) % 2, other

    def piece(t, r, c):
        at = pl.ds(pl.multiple_of((t // PARTS) * ROWS, ROWS), ROWS)
        origin = lax.rem(c + off_ref[r], n_col)
        total = None
        for j in range(n_col):
            gap = origin - j
            weight = jnp.maximum(1 - gap * gap, 0).astype(F32)
            begin = pl.multiple_of(j * w + (t % PARTS) * part, 128)
            term = src[r, at, pl.ds(begin, part)] * jnp.full((ROWS, part), weight, F32).astype(src.dtype)
            total = term if total is None else total + term
        return total.astype(F32)

    def convert(t):
        @pl.when(t % PARTS == 0)
        def _():
            load(t // PARTS).wait()

        @pl.loop(0, blocks)
        def _(i):
            r, yd, other = spot(i)
            v = piece(t, r, yd * 2 + 1 - core)
            send0[t, 0, i] = v[:8]
            send0[t, 1, other] = v[8:]

        for o in range(2):
            copy(0, t, o).start()

    def stage0(t):
        for o in range(2):
            copy(0, t, o).wait_recv()

        @pl.loop(0, blocks)
        def _(i):
            r, yd, other = spot(i)
            v = piece(t, r, yd * 2 + core)
            sums[0][t, 0, i] += v[:8]
            sums[0][t, 1, other] += v[8:]

        for o in range(2):
            copy(1, t, o).start()

    def fold(stage, t):
        for o in range(2):
            copy(stage, t, o).wait_recv()

            @pl.loop(0, blocks >> stage)
            def _(i):
                sums[stage][t, o, i] += sums[stage - 1][t, o, i]

            copy(stage + 1, t, o).start()

    def finish(t):
        for o in range(2):
            copy(bits, t, o).wait_recv()
            v = (sums[bits][t, o, 0] + sums[bits - 1][t, o, 0]) * (1.0 / devices)
            at = pl.ds(pl.multiple_of((t // PARTS) * ROWS + o * 8, 8), 8)
            out_ref[at, pl.ds(pl.multiple_of((t % PARTS) * part, 128), part)] = v
            v = v * v
            total = v[:, 0:128]
            for j in range(128, part, 128):
                total = total + v[:, j : j + 128]
            sq[t % PARTS, at, :] = total

    stages = [convert, stage0]
    stages += [functools.partial(fold, s) for s in range(1, bits)]
    stages += [finish]

    @pl.loop(0, steps + LAG * (len(stages) - 1))
    def _(t):
        for i, stage in enumerate(stages):
            lag = i * LAG

            @pl.when((t >= lag) & (t < steps + lag))
            def _():
                stage(t - lag)

    lane = lax.broadcasted_iota(jnp.int32, (1, 128), 1)
    starts = jnp.zeros((1, 128), jnp.int32)
    lengths = jnp.zeros((1, 128), jnp.int32)
    begin = jnp.int32(0)
    for b in range(len_ref.shape[0]):
        starts = jnp.where(lane == b, begin, starts)
        lengths = jnp.where(lane == b, len_ref[b], lengths)
        begin = begin + len_ref[b]
    ids = lax.broadcasted_iota(jnp.int32, (rows, 128), 0) + row * rows
    after = jnp.clip(ids - starts + 1, 0, 1)
    before = jnp.clip(starts + lengths - ids, 0, 1)
    inside = (after * before).astype(F32)
    row_squares = jnp.sum(jnp.sum(sq[...], axis=0), axis=1, keepdims=True)
    local = jnp.sum(inside * row_squares, axis=0, keepdims=True)
    mine[...] = local
    slots[me] = local

    @pl.loop(1, devices)
    def _(k):
        copya(k).start()

    @pl.loop(0, steps)
    def _(t):
        for o in range(2):
            for s in range(bits + 1):
                copy(s, t, o).wait_send()

    @pl.loop(1, devices)
    def _(k):
        other = (me + devices - k) % devices
        remote(mine, slots.at[other], sa.at[k], ra.at[other], place(k)).wait_recv()
        copya(k).wait_send()

    squares = slots[0]
    for i in range(1, devices):
        squares = squares + slots[i]
    overall = jnp.sqrt(jnp.sum(squares, axis=1, keepdims=True) / (n_row * rows * width))
    clip = clip_ref[0]
    factor = clip / jnp.maximum(overall, clip)
    out_ref[...] = out_ref[...] * factor
    rms = jnp.sqrt(squares / (jnp.maximum(lengths, 1).astype(F32) * width))
    rms_ref[...] = rms[:, : rms_ref.shape[1]]


def shards(n_row, n_col, gradients, bucket_lengths, owner_offset, clip_rms):
    _, total_rows, width = gradients.shape
    rows, w = total_rows // n_row, width // n_col
    devices = n_row * n_col
    steps = rows // ROWS * PARTS
    bits = devices.bit_length() - 2
    blocks = 1 << bits
    vmem, smem = pltpu.VMEM, pltpu.SMEM
    dma = pltpu.SemaphoreType.DMA
    clipped, rms = pl.pallas_call(
        functools.partial(kernel, n_row, n_col, bits),
        out_shape=(
            jax.ShapeDtypeStruct((rows, w), F32),
            jax.ShapeDtypeStruct((1, bucket_lengths.shape[0]), F32),
        ),
        in_specs=[
            pl.BlockSpec(memory_space=pl.ANY),
            pl.BlockSpec(memory_space=smem),
            pl.BlockSpec(memory_space=smem),
            pl.BlockSpec(memory_space=smem),
        ],
        out_specs=[pl.BlockSpec(memory_space=vmem)] * 2,
        scratch_shapes=[
            vmem((n_row, rows, width), gradients.dtype),
            vmem((steps, 2, blocks, 8, w // PARTS), F32),
            *[vmem((steps, 2, blocks >> s, 8, w // PARTS), F32) for s in range(bits + 1)],
            vmem((1, 128), F32),
            vmem((devices, 1, 128), F32),
            vmem((PARTS, rows, 128), F32),
            dma((rows // ROWS,)),
            dma((bits + 1, steps, 2)), dma((bits + 1, steps, 2)),
            dma((devices,)), dma((devices,)),
        ],
        compiler_params=pltpu.CompilerParams(
            collective_id=0, has_side_effects=True, vmem_limit_bytes=60 * 1024 * 1024
        ),
    )(gradients.reshape(n_row, rows, width), bucket_lengths, owner_offset, clip_rms)
    return clipped, rms[0]


def solution(mesh):
    n_row, n_col = mesh.shape["row"], mesh.shape["col"]
    in_specs = (P(("row", "col"), None, None), P(), P(), P())
    out_specs = (P("row", "col"), P())
    return jax.shard_map(
        functools.partial(shards, n_row, n_col),
        mesh=mesh, in_specs=in_specs, out_specs=out_specs, check_vma=False,
    )
```

time: 365 us -> 106 us (0.29)
  waiting for transfers between devices: 227 us -> 0 us
  Pallas kernels: 0 us -> 101 us
  blocking collectives: 42.7 us -> 0 us
  local copies, waits for them, and re-layouts: 42.6 us -> 3.13 us
  other arithmetic: 35.9 us -> 0 us
  between operations: 15.5 us -> 1.29 us
    reduce_scatter x1 -> x0, waiting for transfers between devices: 227 us -> none  [shards(): lax.psum_scatter(blocks, ('row', 'col'), scatter_dimension=0, tiled=True)]
    pallas_call x0 -> x1, Pallas kernels: none -> 101 us  [shards(): pl.pallas_call(functools.partial(kernel, n_row, n_col, bits), out_shape=(...]
    psum x1 -> x0, blocking collectives: 42.7 us -> none  [shards(): bucket_squares = lax.psum(local_squares, ('row', 'col'))]
    another operation x3 -> x0, local copies, waits for them, and re-layouts: 29.3 us -> none  [the longest x2 29.2 us: shards(): blocks = source.reshape(n_row, rows_local, n_col, width_local)]
    concatenate x1 -> x0, other arithmetic: 17.5 us -> none  [turn_block(): return jnp.roll(block, -shift, axis=1)]
    convert_element_type x1 -> x0, other arithmetic: 13.6 us -> none  [shards(): blocks.transpose(0, 2, 1, 3).reshape(devices * rows_local, width_local)]
    gather x1 -> x0, local copies, waits for them, and re-layouts: 12.7 us -> none  [turn_block(): return jnp.roll(block, -shift, axis=1)]
  transfers between devices with their start and end apart: 1 -> 0, of which waited for: 1 -> 0; matrix products, arithmetic and copies ran while one was open for 0% -> 0% of each run, Pallas kernels for 0% -> 0%
where the time goes in v2:
time: 106 us
  Pallas kernels  101 us (95%)
  local copies, waits for them, and re-layouts  3.13 us (3%)
  between operations  1.29 us (1%)
    pallas_call x1, Pallas kernels, shards(): pl.pallas_call(functools.partial(kernel, n_row, n_col, bits), out_shape=(...  101 us
    unnamed x2, local copies, waits for them, and re-layouts  3.13 us

profile of v2, /device:TPU:0, one launch (start us, length us, event | category | flops | bytes accessed | tf_op | source)
XLA Modules:
  0.0 105.5 jit_solution(48192736632954156)
XLA Ops:
  1.3 101.1 %shard_map.59 = (f32[128,1280]{1,0:T(8,128)}, f32[1,16]{1,0:T(1,128)}) custom-call(bf16[8,128,5120]{2,1,0:T(8,128)(2,1)} %bitcast.2, s32[16]{0:T(128)} %len_ref.1, s32[8]{0:T(128)} %off_ref.1, f32[1]{0:T(128)S(6)} %copy.8.clip_ref), custom_call_target="tpu_custom_call" | custom-call | tf_op jit(solution)/shard_map/pallas_call | solution.py:216
  102.4 2.0 %copy.9 = f32[128,1280]{1,0:T(8,128)} copy(f32[128,1280]{1,0:T(8,128)} %get-tuple-element.8) | data formatting | bytes 1310720
  104.4 1.2 %copy.10 = f32[16]{0:T(128)} copy(f32[16]{0:T(128)} %bitcast.3) | data formatting | bytes 128

commit v3 on v2

--- a/solution.py
+++ b/solution.py
@@ -101,7 +101,7 @@
         def _():
             load(t // PARTS).wait()
 
-        @pl.loop(0, blocks)
+        @pl.loop(0, blocks, unroll=2)
         def _(i):
             r, yd, other = spot(i)
             v = piece(t, r, yd * 2 + 1 - core)
@@ -115,7 +115,7 @@
         for o in range(2):
             copy(0, t, o).wait_recv()
 
-        @pl.loop(0, blocks)
+        @pl.loop(0, blocks, unroll=2)
         def _(i):
             r, yd, other = spot(i)
             v = piece(t, r, yd * 2 + core)
@@ -129,7 +129,7 @@
         for o in range(2):
             copy(stage, t, o).wait_recv()
 
-            @pl.loop(0, blocks >> stage)
+            @pl.loop(0, blocks >> stage, unroll=2)
             def _(i):
                 sums[stage][t, o, i] += sums[stage - 1][t, o, i]
 
@@ -238,7 +238,7 @@
             dma((devices,)), dma((devices,)),
         ],
         compiler_params=pltpu.CompilerParams(
-            collective_id=0, has_side_effects=True, vmem_limit_bytes=60 * 1024 * 1024
+            collective_id=0, has_side_effects=True, vmem_limit_bytes=44 * 1024 * 1024
         ),
     )(gradients.reshape(n_row, rows, width), bucket_lengths, owner_offset, clip_rms)
     return clipped, rms[0]

time: 106 us -> 104 us (0.981)
  Pallas kernels: 101 us -> 99.6 us
    pallas_call x1, Pallas kernels: 101 us -> 99.6 us  [shards(): pl.pallas_call(functools.partial(kernel, n_row, n_col, bits), out_shape=(...]
    unnamed x2 -> x6, local copies, waits for them, and re-layouts: 3.13 us -> 2.65 us
where the time goes in v3:
time: 104 us
  Pallas kernels  99.6 us (96%)
  local copies, waits for them, and re-layouts  2.65 us (3%)
  between operations  1.29 us (1%)
    pallas_call x1, Pallas kernels, shards(): pl.pallas_call(functools.partial(kernel, n_row, n_col, bits), out_shape=(...  99.6 us
    unnamed x6, local copies, waits for them, and re-layouts  2.65 us

profile of v3, /device:TPU:0, one launch (start us, length us, event | category | flops | bytes accessed | tf_op | source)
XLA Modules:
  0.0 103.6 jit_solution(18060449003131333409)
XLA Ops:
  1.3 0.0 copy-start
  1.3 0.6 copy-done
  1.9 0.0 copy-start.1
  1.9 0.7 copy-done.1
  2.6 99.6 %shard_map.59 = (f32[128,1280]{1,0:T(8,128)S(1)}, f32[1,16]{1,0:T(1,128)S(1)}) custom-call(bf16[8,128,5120]{2,1,0:T(8,128)(2,1)} %bitcast.3, s32[16]{0:T(128)S(1)} %copy-done, s32[8]{0:T(128)S(1)} %copy-done.1, f32[1]{0:T(128)S(6)} %copy.8.clip_ref), custom_call_target="tpu_custom_call" | custom-call | tf_op jit(solution)/shard_map/pallas_call | solution.py:216
  102.2 0.8 copy.9
  103.1 0.5 copy.10
Async XLA Ops:
  1.3 0.7 copy-start
  1.9 0.7 copy-start.1
